TPU v7x, 32 devices: a whole 2x2x4 slice. The times are simulated.
32 devices in a mesh: tp: 8 (over z, y), ep: 4 (over x, core).
Axes of the slice: x: 2, y: 2, z: 4, core: 2. Of those that a mesh axis runs over, the one named last changes fastest.
Arguments:
- x: bfloat16 [16384, 2048], P(('ep', 'tp'))
- idx: int32 [16384, 4], P(('ep', 'tp'))
- g: float32 [16384, 4], P(('ep', 'tp'))
- slot: int32 [16384, 4], P(('ep', 'tp'))
- ws1: bfloat16 [2048, 5632], P(None, 'tp')
- ws3: bfloat16 [2048, 5632], P(None, 'tp')
- ws2: bfloat16 [5632, 2048], P('tp')
- w1: bfloat16 [60, 2048, 1408], P('ep')
- w3: bfloat16 [60, 2048, 1408], P('ep')
- w2: bfloat16 [60, 1408, 2048], P('ep')
Outputs:
- output: bfloat16 [16384, 2048], P(('ep', 'tp'))
All inputs are finite; a program needn't handle non-finite values.
Results may differ from a plain program's by a relative error of at most 0.001.
Values are sent between devices in bfloat16 or wider.
A program may use at most 1.25 GiB of HBM per device.

v0:
```python
import jax
import jax.numpy as jnp
from jax import lax
from jax.sharding import PartitionSpec as P


def _swiglu2(x, w1, w3, w2):
    a = jnp.dot(x, w1, preferred_element_type=jnp.float32)
    b = jnp.dot(x, w3, preferred_element_type=jnp.float32)
    h = (jax.nn.silu(a) * b).astype(jnp.bfloat16)
    return jnp.dot(h, w2, preferred_element_type=jnp.float32)


def _experts(xs, w1, w3, w2):
    a = jnp.einsum("erd,edf->erf", xs, w1, preferred_element_type=jnp.float32)
    b = jnp.einsum("erd,edf->erf", xs, w3, preferred_element_type=jnp.float32)
    h = (jax.nn.silu(a) * b).astype(jnp.bfloat16)
    return jnp.einsum("erf,efd->erd", h, w2, preferred_element_type=jnp.float32).astype(jnp.bfloat16)


def _routed(x, idx, g, slot, w1, w3, w2, ep):
    tok, d = x.shape
    k = idx.shape[1]
    el = w1.shape[0]
    e = el * ep
    cap = max(8, (2 * tok * k + 8 * e - 1) // (8 * e) * 8)
    kept = slot >= 0
    pos = jnp.where(kept, idx * cap + slot, e * cap)
    send = jnp.zeros((e * cap, d), jnp.bfloat16).at[pos.reshape(-1)].set(jnp.repeat(x, k, axis=0), mode="drop")
    recv = lax.all_to_all(send.reshape(ep, el, cap, d), "ep", 0, 0, tiled=True)
    xs = jnp.swapaxes(recv, 0, 1).reshape(el, ep * cap, d)
    out = jnp.swapaxes(_experts(xs, w1, w3, w2).reshape(el, ep, cap, d), 0, 1)
    back = lax.all_to_all(out, "ep", 0, 0, tiled=True).reshape(e * cap, d)
    r = jnp.take(back, jnp.where(kept, pos, 0), axis=0)
    gate = jnp.where(kept, g, 0.0)
    acc = jnp.zeros((tok, d), jnp.float32)
    for j in range(k):
        acc = acc + gate[:, j:j + 1] * r[:, j].astype(jnp.float32)
    return acc


def solution(mesh):
    ep = mesh.shape["ep"]
    rows = P(("ep", "tp"), None)

    def body(x, idx, g, slot, ws1, ws3, ws2, w1, w3, w2):
        xg = lax.all_gather(x, "tp", axis=0, tiled=True)
        s = lax.psum_scatter(_swiglu2(xg, ws1, ws3, ws2), "tp", scatter_dimension=0, tiled=True)
        r = _routed(x, idx, g, slot, w1, w3, w2, ep)
        return (x.astype(jnp.float32) + s + r).astype(jnp.bfloat16)

    return jax.shard_map(
        body, mesh=mesh,
        in_specs=(rows, rows, rows, rows, P(None, "tp"), P(None, "tp"), P("tp", None),
                  P("ep", None, None), P("ep", None, None), P("ep", None, None)),
        out_specs=rows, check_vma=False)
```

profile of v0, /device:TPU:0, one launch (start us, length us, event | category | flops | bytes accessed | tf_op | source)
XLA Modules:
  0.0 966.0 jit_solution(17011095630311815424)
XLA Ops:
  6.5 0.0 all-gather.2.cloned.1.call-start
  6.5 0.7 all-gather.2.cloned.1.call-update
  7.3 0.0 reduce-scatter.2.cloned.1.call-start
  7.3 231.6 %all-gather.2.cloned.1.call-done = bf16[4096,2048]{1,0:T(8,128)(2,1)} async-done(((bf16[512,2048]{1,0:T(8,128)(2,1)}), bf16[4096,2048]{1,0:T(8,128)(2,1)}) %all-gather.2.cloned.1.call-update) | async-done | bytes 16777232 | tf_op jit(solution)/shard_map/all_gather | solution.py:47
  238.9 19.0 %fusion.11 = f32[4096,704]{0,1:T(8,128)} fusion(bf16[4096,2048]{1,0:T(8,128)(2,1)} %all-gather.2.cloned.1.call-done, bf16[2048,704]{0,1:T(8,128)(2,1)} %param.14), kind=kOutput, calls=%fused_computation.33 | convolution fusion | flops 11811160064 | bytes 31195136 | tf_op jit(solution)/shard_map/dot_general | solution.py:8
  257.9 0.0 copy-done
  257.9 33.6 %fusion.2 = f32[4096,2048]{1,0:T(8,128)} fusion(bf16[704,2048]{1,0:T(8,128)(2,1)S(1)} %copy-done, f32[4096,704]{0,1:T(8,128)} %fusion.11, bf16[4096,2048]{1,0:T(8,128)(2,1)} %all-gather.2.cloned.1.call-done, bf16[2048,704]{0,1:T(8,128)(2,1)} %param.15), kind=kOutput, calls=%fused_computation.9 | convolution fusion | flops 23639621632 | bytes 67633152 | tf_op jit(solution)/shard_map/dot_general | solution.py:11
  291.5 0.0 reduce-scatter.2.cloned.1.call-update
  291.5 0.7 copy-done.3
  292.1 0.0 copy-done.5
  292.2 0.1 copy.17
  292.3 0.2 reshape.59
  292.5 0.6 copy-done.2
  293.1 6.5 broadcast_in_dim.32
  299.6 12.6 %reshape.81 = bf16[2048,2048]{1,0:T(8,128)(2,1)} reshape(bf16[512,4,2048]{2,1,0:T(4,128)(2,1)} %broadcast_in_dim.32) | data formatting | bytes 16777216 | tf_op jit(solution)/shard_map/reshape | solution.py:29
  312.3 22.8 %scatter_custom_fusion = bf16[4320,2048]{1,0:T(8,128)(2,1)} fusion(s32[2048]{0:T(1024)S(1)} %bitcast.69, bf16[2048,2048]{1,0:T(8,128)(2,1)} %reshape.81, bf16[]{:T(256)} %constant.16.clone.1), kind=kCustom, calls=%fused_computation.6 | custom fusion | bytes 17695232 | tf_op jit(solution)/shard_map/scatter | solution.py:29
  335.1 197.6 %all_to_all.10 = bf16[4,15,72,2048]{3,2,1,0:T(8,128)(2,1)S(1)} all-to-all(bf16[4,15,72,2048]{3,2,1,0:T(8,128)(2,1)} %bitcast.63), channel_id=1, replica_groups=mesh['tp'=8,'ep'=4] {'ep'}, dimensions={0} | all-to-all | bytes 35389440 | tf_op jit(solution)/shard_map/all_to_all | solution.py:30
  532.7 7.2 copy.18
  539.9 47.2 %fusion.12 = f32[15,288,1408]{2,1,0:T(8,128)} fusion(bf16[15,288,2048]{2,1,0:T(8,128)(2,1)} %bitcast.66, bf16[15,2048,1408]{2,1,0:T(8,128)(2,1)} %param.17), kind=kOutput, calls=%fused_computation.34 | convolution fusion | flops 24914165760 | bytes 128532480 | tf_op jit(solution)/shard_map/erd,edf->erf/dot_general | solution.py:15
  587.0 48.6 %fusion.41 = bf16[15,288,1408]{2,1,0:T(8,128)(2,1)} fusion(bf16[15,2048,1408]{2,1,0:T(8,128)(2,1)} %param.18, bf16[15,288,2048]{2,1,0:T(8,128)(2,1)} %bitcast.67, f32[15,288,1408]{2,1,0:T(8,128)} %fusion.12), kind=kOutput, calls=%bitcast_fusion.1.clone.1 | convolution fusion | flops 24950661120 | bytes 140697600 | tf_op jit(solution)/shard_map/erd,edf->erf/dot_general | solution.py:16
  635.7 43.9 %convolution_convert_fusion = bf16[15,288,2048]{2,1,0:T(8,128)(2,1)} fusion(bf16[15,1408,2048]{2,1,0:T(8,128)(2,1)} %param.19, bf16[15,288,1408]{2,1,0:T(8,128)(2,1)} %fusion.41), kind=kOutput, calls=%fused_computation.4 | convolution fusion | flops 24923013120 | bytes 116367360 | tf_op jit(solution)/shard_map/erf,efd->erd/dot_general | solution.py:18
  679.5 16.2 %copy.24 = bf16[15,4,72,2048]{3,2,0,1:T(8,128)(2,1)} copy(bf16[15,4,72,2048]{3,2,1,0:T(8,128)(2,1)} %bitcast.68) | data formatting | bytes 35389440 | tf_op jit(solution)/shard_map/reshape | solution.py:32
  695.7 7.6 all-to-all-start.1
  703.3 0.0 copy-done.4
  703.4 0.0 copy-done.6
  703.4 0.1 copy.20
  703.5 0.2 reshape.71
  703.8 192.1 %all-to-all-done.1 = bf16[4,15,72,2048]{3,2,1,0:T(8,128)(2,1)} async-done(((bf16[4,15,72,2048]{3,2,1,0:T(8,128)(2,1)}), bf16[4,15,72,2048]{3,2,1,0:T(8,128)(2,1)}, u32[]{:S(2)}, u32[]{:S(2)}) %all-to-all-start.1) | async-done | bytes 17694752 | tf_op jit(solution)/shard_map/all_to_all | solution.py:33
  895.9 24.6 %gather_fusion = bf16[2048,2048]{1,0:T(8,128)(2,1)} fusion(bf16[4320,2048]{1,0:T(8,128)(2,1)} %bitcast.7, s32[2048]{0:T(1024)S(1)} %broadcast_clamp_fusion), kind=kCustom, calls=%fused_computation | custom fusion | bytes 16785408 | tf_op jit(solution)/shard_map/jit(_take)/gather | solution.py:34
  920.5 13.1 %reshape.70 = bf16[512,4,2048]{2,1,0:T(4,128)(2,1)} reshape(bf16[2048,2048]{1,0:T(8,128)(2,1)} %gather_fusion) | data formatting | bytes 16777216 | tf_op jit(solution)/shard_map/jit(_take)/gather | solution.py:34
  933.6 17.8 %copy_select_fusion = bf16[512,4,2048]{2,0,1:T(8,128)(2,1)} fusion(bf16[512,4,2048]{2,1,0:T(4,128)(2,1)} %reshape.70, pred[512,4]{0,1:T(4,128)(4,1)S(1)} %get-tuple-element.5), kind=kLoop, calls=%fused_computation.8 | loop fusion | flops 4194304 | bytes 16779264 | tf_op jit(solution)/shard_map/jit(_take)/select_n | solution.py:34
  951.4 7.3 fusion.6
  (17 shorter events, 0.1 us)
Async XLA Ops:
  6.5 251.3 %copy-start = (bf16[704,2048]{1,0:T(8,128)(2,1)S(1)}, bf16[704,2048]{1,0:T(8,128)(2,1)}, u32[]{:S(2)}) copy-start(bf16[704,2048]{1,0:T(8,128)(2,1)} %param.16) | copy-start | bytes 8650756
  6.5 232.4 %all-gather.2.cloned.1.call-start = ((), (), s32[]{:S(2)}) async-start(), calls=%async_computation.3 | async-start | bytes 18874368 | tf_op jit(solution)/shard_map/all_gather | solution.py:47
  7.3 944.1 %reduce-scatter.2.cloned.1.call-start = ((), (), s32[]{:S(2)}) async-start(), calls=%async_computation.4 | async-start | bytes 37748736 | tf_op jit(solution)/shard_map/reduce_scatter | solution.py:48
  291.4 0.7 copy-start.3
  291.4 0.7 copy-start.5
  291.5 1.6 copy-start.2
  695.7 7.7 copy-start.4
  695.7 7.7 copy-start.6
  695.7 8.0 copy-start.7
  695.7 200.2 %all-to-all-start.1 = ((bf16[4,15,72,2048]{3,2,1,0:T(8,128)(2,1)}), bf16[4,15,72,2048]{3,2,1,0:T(8,128)(2,1)}, u32[]{:S(2)}, u32[]{:S(2)}) async-start(bf16[4,15,72,2048]{3,2,1,0:T(8,128)(2,1)} %bitcast.64), calls=%async_computation.2 | async-start | bytes 35389440 | tf_op jit(solution)/shard_map/all_to_all | solution.py:33
  933.6 25.1 %copy-start.1 = (bf16[704,2048]{1,0:T(8,128)(2,1)S(1)}, bf16[704,2048]{1,0:T(8,128)(2,1)}, u32[]{:S(2)}) copy-start(bf16[704,2048]{1,0:T(8,128)(2,1)} %param.16) | copy-start | bytes 8650756
Sparse Core Ops, SparseCore 0:
  9.5 229.4 all-gather.1
  291.6 532.3 reduce-scatter.1
where the time goes:
time: 975 us; the launch traced here: 966 us
  waiting for transfers between devices  424 us (43%)
  blocking collectives  198 us (20%)
  matrix products  192 us (20%)
  local copies, waits for them, and re-layouts  105 us (11%)
  other arithmetic  25.2 us (3%)
  between operations  14 us (1%)
    all_gather x1, waiting for transfers between devices, body(): xg = lax.all_gather(x, 'tp', axis=0, tiled=True)  232 us
    all_to_all x1, blocking collectives, _routed(): recv = lax.all_to_all(send.reshape(ep, el, cap, d), 'ep', 0, 0, tiled=True)  198 us
    all_to_all x1, waiting for transfers between devices, _routed(): back = lax.all_to_all(out, 'ep', 0, 0, tiled=True).reshape(e * cap, d)  192 us
    dot_general x1, matrix products, _experts(): b = jnp.einsum('erd,edf->erf', xs, w3, preferred_element_type=jnp.float32)  48.6 us
    dot_general x1, matrix products, _experts(): a = jnp.einsum('erd,edf->erf', xs, w1, preferred_element_type=jnp.float32)  47.2 us
    dot_general x1, matrix products, _experts(): jnp.einsum('erf,efd->erd', h, w2, preferred_element_type=jnp.float32)  43.9 us
    gather x2, local copies, waits for them, and re-layouts, _routed(): r = jnp.take(back, jnp.where(kept, pos, 0), axis=0)  37.7 us
    dot_general x1, matrix products, _swiglu2(): return jnp.dot(h, w2, preferred_element_type=jnp.float32)  33.6 us
  transfers between devices with their start and end apart: 3, of which 2 were waited for; matrix products, arithmetic and copies ran while one was open for 27% of the time, Pallas kernels for 0%

commit v1 on v0

v1 whole, which is shorter than its diff:
```python
import functools

import jax
import jax.numpy as jnp
from jax import lax
from jax.experimental import pallas as pl
from jax.experimental.pallas import tpu as pltpu
from jax.sharding import PartitionSpec as P


F32, BF16, I32 = jnp.float32, jnp.bfloat16, jnp.int32
D = 2048
TOK = 512
EL = 15
F = 1408
CAP = 72
MP = 4 * CAP
EG = 3
SUB = 176
GRP = 384
DB = 1024
LT = DB // 128
PITCH = LT + 1
ACC = (TOK + 1) * LT

CORE = [(0, 1), (1, 0), (2, 3), (3, 2)]
XSW = [(0, 2), (1, 3), (2, 0), (3, 1)]
YSW = [(p, p ^ 1) for p in range(8)]

HBM = pl.BlockSpec(memory_space=pl.ANY)


def _params(vmem=60, **more):
    return pltpu.CompilerParams(vmem_limit_bytes=vmem << 20, **more)


def _cost(flops, nbytes):
    return pl.CostEstimate(flops=int(flops), bytes_accessed=int(nbytes), transcendentals=0)


def _silu_mul(a, b):
    return a * jax.nn.sigmoid(a) * b


def _copy(src, dst, sem):
    return pltpu.make_async_copy(src, dst, sem)


RING = 5


def _front_kernel(x, meta, w13, wq2, w1, w3, h, hs, w2a, w2b, lists,
                  xv, mv, wv, lhs, hv, wg, sv, bounce,
                  xsem, msem, wsem, hsem, ssem, lsem, bsem, xsend, xrecv, msend, mrecv, wsend, wrecv, asend, arecv, csend, crecv):
    tp, q = lax.axis_index("tp"), lax.axis_index("ep")
    z = tp // 2
    mid = (z == 1) | (z == 2)
    end = (z == 0) | (z == 3)
    near = {"ep": q + 1 - 2 * lax.rem(q, 2)}
    far = {"ep": lax.rem(q + 2, 4)}
    other = {"tp": tp + 1 - 2 * lax.rem(tp, 2)}
    pair = {"tp": tp + 2 - 4 * lax.rem(z, 2)}
    across = {"tp": lax.rem(tp, 2) + 2 * (3 - z)}

    barrier = pltpu.get_barrier_semaphore()
    for d in (near, far, other, pair):
        pl.semaphore_signal(barrier, inc=1, device_id=d, device_id_type=pl.DeviceIdType.MESH)
    pl.when(mid)(lambda: pl.semaphore_signal(barrier, inc=1, device_id=across, device_id_type=pl.DeviceIdType.MESH))
    pl.semaphore_wait(barrier, 4 + z * (3 - z) // 2)

    def remote(src, dst, send, recv, device):
        return pltpu.make_async_remote_copy(src_ref=src, dst_ref=dst, send_sem=send, recv_sem=recv, device_id=device,
                                            device_id_type=pl.DeviceIdType.MESH)

    m_near = remote(meta, mv.at[1], msend.at[0], mrecv.at[1], near)
    m_far = remote(meta, mv.at[2], msend.at[1], mrecv.at[2], far)
    m_cross = remote(mv.at[2], mv.at[3], msend.at[2], mrecv.at[3], near)
    x_near = remote(x, xv.at[1], xsend.at[0], xrecv.at[1], near)
    x_far = remote(x, xv.at[2], xsend.at[1], xrecv.at[2], far)
    x_cross = remote(xv.at[2], xv.at[3], xsend.at[2], xrecv.at[3], near)
    x_own = _copy(x, xv.at[0], xsem.at[0])
    m_own = _copy(meta, mv.at[0], msem.at[0])

    def up(src, slot, n, device):
        return remote(src, wg.at[slot], wsend.at[n], wrecv.at[slot], device)

    u_y = [up(w13 if k == 0 else wg.at[2 * k], 2 * k + 1, k, other) for k in range(4)]
    u_pair = {0: up(w13, 2, 4, pair), 2: up(wg.at[4], 4, 5, pair), 3: up(wg.at[6], 6, 6, pair)}
    u_mid = {0: up(w13, 4, 7, across), 1: up(wg.at[2], 6, 8, across)}
    u_own = _copy(w13, wg.at[0], lsem.at[0])

    def down(src, slot, n, device):
        return remote(src, w2a.at[slot], asend.at[n], arecv.at[slot], device)

    def later(src, slot, n, device):
        return remote(src, w2b.at[slot], csend.at[n], crecv.at[slot], device)

    wa, wb = wq2.at[0], wq2.at[1]
    a_y = [down(wa if k == 0 else w2a.at[2 * k], 2 * k + 1, k, other) for k in range(4)]
    a_pair = {0: down(wa, 2, 4, pair), 2: down(w2a.at[4], 4, 5, pair), 3: down(w2a.at[6], 6, 6, pair)}
    a_mid = {0: down(wa, 4, 7, across), 1: down(w2a.at[2], 6, 8, across)}
    c_pair = {0: later(wb, 1, 0, pair), 2: later(w2b.at[2], 2, 1, pair), 3: later(w2b.at[3], 3, 2, pair)}
    c_mid = {0: later(wb, 2, 3, across), 1: later(w2b.at[1], 3, 4, across)}
    got = lambda c: c.wait_recv()

    for c in (m_near, m_far, x_near, x_far, u_y[0], u_pair[0]):
        c.start()
    pl.when(mid)(u_mid[0].start)

    @pl.when(end)
    def _():
        a_pair[0].start()
        c_pair[0].start()

    for c in (m_own, x_own, u_own):
        c.start()

    def weights(m):
        slot, e = lax.rem(m, RING), m // 2

        def either(what):
            pl.when(lax.rem(m, 2) == 0)(lambda: what(_copy(w1.at[e], wv.at[slot], wsem.at[slot])))
            pl.when(lax.rem(m, 2) == 1)(lambda: what(_copy(w3.at[e], wv.at[slot], wsem.at[slot])))

        return either

    for m in range(RING):
        weights(m)(lambda c: c.start())
    b_in, b_out = _copy(wb, bounce, bsem.at[0]), _copy(bounce, w2b.at[0], bsem.at[1])
    b_in.start()
    m_own.wait()
    x_own.wait()
    got(m_far)
    m_cross.start()
    got(m_near)
    got(m_cross)
    b_in.wait()
    b_out.start()

    got(u_pair[0])
    u_y[1].start()

    @pl.when(mid)
    def _():
        u_mid[1].start()
        got(u_mid[0])
        u_pair[2].start()
        u_y[2].start()

    got(x_near)
    got(x_far)
    x_cross.start()
    got(x_cross)

    def second():
        @pl.when(end)
        def _():
            got(u_pair[2])
            u_y[2].start()

        @pl.when(mid)
        def _():
            got(u_mid[1])
            u_pair[3].start()
            u_y[3].start()
            a_mid[0].start()
            a_pair[0].start()
            got(a_pair[0])
            a_mid[1].start()
            c_mid[0].start()
            c_pair[0].start()
            got(c_pair[0])
            c_mid[1].start()

    def third():
        @pl.when(end)
        def _():
            got(u_pair[3])
            u_y[3].start()
            a_y[0].start()

        @pl.when(mid)
        def _():
            a_y[0].start()
            a_y[1].start()
            got(a_mid[0])
            a_pair[2].start()
            a_y[2].start()
            got(a_mid[1])
            a_pair[3].start()
            a_y[3].start()
            got(c_mid[0])
            c_pair[2].start()
            got(c_mid[1])
            c_pair[3].start()

    def fourth():
        @pl.when(end)
        def _():
            for k, c in ((1, a_pair[0]), (2, a_pair[2]), (3, a_pair[3])):
                got(c)
                a_y[k].start()

    rows = EG * CAP
    row = lax.broadcasted_iota(I32, (rows, TOK), 0).astype(F32)
    tok = lax.broadcasted_iota(I32, (rows, TOK), 1).astype(F32) - float(TOK)
    lane = lax.broadcasted_iota(I32, (rows, 128), 1)

    def group(k, carry):
        first = (q * EL * CAP + k * rows).astype(F32)
        at = pl.ds(pl.multiple_of(k * rows, 8), rows)

        def half(p, cols):
            hots = []
            for j in range(2):
                s = 2 * p + j
                gate = jnp.zeros((rows, TOK), F32)
                for i in range(4):
                    gate = gate + jnp.where(mv[s, i:i + 1, :] - first == row, mv[s, 4 + i:5 + i, :], 0.0)
                hit = gate > 0.0
                hots.append(jnp.where(hit, 1.0, 0.0).astype(BF16))
                t = jnp.sum(jnp.where(hit, tok, 0.0), axis=1, keepdims=True) + float(TOK)
                gt = jnp.sum(gate, axis=1, keepdims=True)
                cols = jnp.where(lane == s, t, jnp.where(lane == 4 + s, gt, cols))
            to = pl.ds(pl.multiple_of(p * 2 * CAP, 16), 2 * CAP)
            for n in range(0, D, 256):
                r = [jnp.dot(hots[j], xv[2 * p + j, :, n:n + 256], preferred_element_type=F32) for j in range(2)]
                for e in range(EG):
                    lhs[e, to, n:n + 256] = jnp.concatenate(
                        [r[0][e * CAP:(e + 1) * CAP], r[1][e * CAP:(e + 1) * CAP]], axis=0).astype(BF16)
            return cols

        lists[at, :] = lax.fori_loop(0, 2, half, jnp.zeros((rows, 128), F32))

        def expert(e3, carry):
            e = k * EG + e3
            slot0, slot1, out = lax.rem(2 * e, RING), lax.rem(2 * e + 1, RING), lax.rem(e, 2)
            weights(2 * e)(lambda c: c.wait())
            weights(2 * e + 1)(lambda c: c.wait())
            pl.when(e >= 2)(lambda: _copy(hv.at[out], h.at[e - 2], hsem.at[out]).wait())
            a = lhs[e3]
            for n in range(0, F, 128):
                w = jnp.concatenate([wv[slot0, :, n:n + 128], wv[slot1, :, n:n + 128]], axis=1)
                r = jnp.dot(a, w, preferred_element_type=F32)
                hv[out, :, n:n + 128] = _silu_mul(r[:, :128], r[:, 128:]).astype(BF16)
            _copy(hv.at[out], h.at[e], hsem.at[out]).start()
            for m in range(2):
                pl.when(2 * e + RING + m < 2 * EL)(lambda m=m: weights(2 * e + RING + m)(lambda c: c.start()))
            return carry

        lax.fori_loop(0, EG, expert, 0)
        pl.when(k == 0)(second)
        pl.when(k == 2)(third)
        return carry

    lax.fori_loop(0, EL // EG, group, 0)
    fourth()

    half = TOK // 2
    u_own.wait()

    def block(j, carry):
        k, i = j // 8, lax.rem(j, 8)
        for kk in range(4):
            pl.when(j == 8 * kk)(lambda kk=kk: got(u_y[kk]))
        slot = lax.rem(j, 2)
        pl.when(j >= 2)(lambda: _copy(sv.at[slot], hs.at[0, pl.ds(0, half)], ssem.at[slot]).wait())
        a = xv[i // 2, pl.ds(pl.multiple_of(lax.rem(i, 2) * half, half), half), :]
        pad = jnp.zeros((GRP - 2 * SUB, D), BF16)
        w = jnp.concatenate([wg[2 * k, :SUB, :], wg[2 * k + 1, :SUB, :], pad, wg[2 * k, SUB:, :], wg[2 * k + 1, SUB:, :], pad], axis=0)
        r = lax.dot_general(a, w, (((1,), (1,)), ((), ())), preferred_element_type=F32)
        sv[slot] = _silu_mul(r[:, :GRP], r[:, GRP:]).astype(BF16)
        _copy(sv.at[slot], hs.at[k, pl.ds(pl.multiple_of(i * half, half), half)], ssem.at[slot]).start()
        return carry

    lax.fori_loop(0, 32, block, 0)

    for slot in range(2):
        _copy(sv.at[slot], hs.at[0, pl.ds(0, half)], ssem.at[slot]).wait()
        _copy(hv.at[slot], h.at[0], hsem.at[slot]).wait()
    for c in a_y:
        got(c)

    @pl.when(end)
    def _():
        for c in (c_pair[0], c_pair[2], c_pair[3]):
            got(c)

    b_out.wait()
    for c in [m_near, m_far, m_cross, x_near, x_far, x_cross] + u_y + a_y + [u_pair[0], a_pair[0], c_pair[0]]:
        c.wait_send()

    @pl.when(mid)
    def _():
        for c in (u_mid[0], u_mid[1], u_pair[2], u_pair[3], a_mid[0], a_mid[1], a_pair[2], a_pair[3],
                  c_mid[0], c_mid[1], c_pair[2], c_pair[3]):
            c.wait_send()


def _front(x, meta, w13, wq2, w1, w3):
    dma = pltpu.SemaphoreType.DMA
    vmem = pltpu.VMEM
    return pl.pallas_call(
        _front_kernel,
        in_specs=[HBM] * 6,
        out_specs=[HBM] * 4 + [pl.BlockSpec(memory_space=pltpu.VMEM)],
        out_shape=[jax.ShapeDtypeStruct((EL, MP, F), BF16), jax.ShapeDtypeStruct((4, 4 * TOK, GRP), BF16),
                   jax.ShapeDtypeStruct((8, SUB, DB), BF16), jax.ShapeDtypeStruct((4, SUB, DB), BF16),
                   jax.ShapeDtypeStruct((EL * CAP, 128), F32)],
        scratch_shapes=[vmem((4, TOK, D), BF16), vmem((4, 8, TOK), F32), vmem((RING, D, F), BF16), vmem((EG, MP, D), BF16),
                        vmem((2, MP, F), BF16), vmem((8, 2 * SUB, D), BF16), vmem((2, TOK // 2, GRP), BF16), vmem((SUB, DB), BF16),
                        dma((1,)), dma((1,)), dma((RING,)), dma((2,)), dma((2,)), dma((1,)), dma((2,)),
                        dma((3,)), dma((4,)), dma((3,)), dma((4,)), dma((9,)), dma((8,)), dma((9,)), dma((8,)), dma((5,)), dma((4,))],
        compiler_params=_params(collective_id=1, has_side_effects=True),
        cost_estimate=_cost(EL * 2 * MP * D * 2 * F + 2 * 4 * TOK * D * 8 * GRP, EL * 4 * D * F),
        name="front",
    )(x, meta, w13, wq2, w1, w3)


WRING = 8
HRING = 6


def _down_kernel(c, tok, gate, hs, w_own, *rest):
    ws, (h, w2, own, near, far, cross), scratch = rest[:2 - (c == 0)], rest[2 - (c == 0):8 - (c == 0)], rest[8 - (c == 0):]
    sv, wsq, acc, res, wv, hv, ssem, qsem, wsem, hsem, osem = scratch
    rows = TOK // 2
    cols = pl.ds(c * DB, DB)

    def weights(k):
        slot = lax.rem(k, WRING)
        return _copy(w2.at[k, :, cols], wv.at[slot], wsem.at[slot])

    def hidden(k):
        slot = lax.rem(k, HRING)
        return _copy(h.at[k], hv.at[slot], hsem.at[slot])

    loads = []
    for k in range(4):
        for j in range(2):
            if k == 0 and j == 0:
                src = w_own.at[c]
            else:
                src = ws[0].at[2 * k + j] if c == 0 else ws[j].at[k]
            loads.append(_copy(src, wsq.at[pl.ds(k * GRP + j * SUB, SUB)], qsem.at[2 * k + j]))
    halves = []
    for b in range(2):
        at = pl.ds(b * 2 * TOK, 2 * TOK)
        halves.append([_copy(hs.at[k, at], sv.at[k, at], ssem.at[b, k]) for k in range(4)])
    for x in loads + halves[0] + halves[1]:
        x.start()
    for k in range(WRING):
        weights(k).start()
    for k in range(HRING):
        hidden(k).start()
    for k in range(4):
        wsq[k * GRP + 2 * SUB:(k + 1) * GRP, :] = jnp.zeros((GRP - 2 * SUB, DB), BF16)
    for x in loads:
        x.wait()

    def shared(i, carry):
        at = pl.ds(pl.multiple_of(i * rows, rows), rows)
        a = jnp.concatenate([sv[k, at, :] for k in range(4)], axis=1)
        base = pl.multiple_of(i // 2 * ACC + lax.rem(i, 2) * (rows * LT), 8)
        for n in range(0, DB, 256):
            r = jnp.dot(a, wsq[:, n:n + 256], preferred_element_type=F32)
            for j in range(2):
                for b in range(rows // 8):
                    acc[pl.ds(base + b * 8 * LT + n // 128 + j, 8, stride=LT), :] = r[8 * b:8 * b + 8, 128 * j:128 * j + 128]
        return carry

    for b in range(2):
        for x in halves[b]:
            x.wait()
        lax.fori_loop(4 * b, 4 * b + 4, shared, 0)

    def expert(e, carry):
        weights(e).wait()
        hidden(e).wait()
        wslot, hslot = lax.rem(e, WRING), lax.rem(e, HRING)
        a = hv[hslot]
        for n in range(0, DB, 256):
            r = jnp.dot(a, wv[wslot, :, n:n + 256], preferred_element_type=F32).astype(BF16).astype(F32)
            for j in range(2):
                for b in range(MP // 8):
                    res[pl.ds(b * 8 * PITCH + n // 128 + j, 8, stride=PITCH), :] = r[8 * b:8 * b + 8, 128 * j:128 * j + 128]

        @pl.when(e + WRING < EL)
        def _():
            weights(e + WRING).start()

        @pl.when(e + HRING < EL)
        def _():
            hidden(e + HRING).start()

        for s in range(4):
            def step(k, carry, s=s):
                new = []
                for u in range(8):
                    j = ((e * CAP + k * 8 + u) * 4) + s
                    t = pl.multiple_of(s * ACC + tok[j] * LT, LT)
                    row = res[pl.ds((s * CAP + k * 8 + u) * PITCH, LT), :]
                    new.append((t, acc[pl.ds(t, LT), :] + gate[j] * row))
                for t, v in new:
                    acc[pl.ds(t, LT), :] = v
                return carry

            lax.fori_loop(0, CAP // 8, step, 0)
        return carry

    lax.fori_loop(0, EL, expert, 0)
    outs = [_copy(acc.at[pl.ds(k * ACC, ACC)], o, osem.at[k]) for k, o in ((3, cross), (2, far), (1, near), (0, own))]
    for x in outs:
        x.start()
    for x in outs:
        x.wait()


def _down(c, tok, gate, hs, w_own, ws, h, w2):
    dma = pltpu.SemaphoreType.DMA
    return pl.pallas_call(
        functools.partial(_down_kernel, c),
        grid_spec=pltpu.PrefetchScalarGridSpec(
            num_scalar_prefetch=2,
            grid=(1,),
            in_specs=[HBM] * (4 + len(ws)),
            out_specs=[HBM] * 4,
            scratch_shapes=[pltpu.VMEM((4, 4 * TOK, GRP), BF16), pltpu.VMEM((4 * GRP, DB), BF16), pltpu.VMEM((4 * ACC, 128), F32),
                            pltpu.VMEM((MP * PITCH, 128), F32), pltpu.VMEM((WRING, F, DB), BF16), pltpu.VMEM((HRING, MP, F), BF16),
                            dma((2, 4)), dma((8,)), dma((WRING,)), dma((HRING,)), dma((4,))],
        ),
        out_shape=[jax.ShapeDtypeStruct((ACC, 128), F32)] * 4,
        compiler_params=_params(),
        cost_estimate=_cost(2 * 4 * TOK * 4 * GRP * DB + EL * 2 * MP * F * DB, EL * 2 * F * DB),
        name="down",
    )(tok, gate, hs, w_own, *ws, h, w2)


FR = 128


def _final_kernel(c, x, own, near, far, *rest):
    y, xv, tv, yv, xsem, tsem, ysem = rest[-7:]
    cols = pl.ds(c * DB, DB)
    n = TOK // FR

    def loads(k):
        at = pl.ds(k * FR * LT, FR * LT)
        return [_copy(x.at[pl.ds(k * FR, FR), cols], xv.at[k], xsem.at[k])] + [
            _copy(t.at[at], tv.at[k, j], tsem.at[k, j]) for j, t in enumerate((own, near, far))]

    def store(k):
        return _copy(yv.at[k], y.at[pl.ds(k * FR, FR), cols], ysem.at[k])

    for k in range(n):
        for m in loads(k):
            m.start()

    for k in range(n):
        for m in loads(k):
            m.wait()
        for b in range(FR // 8):
            for l in range(LT):
                at = pl.ds(b * 8 * LT + l, 8, stride=LT)
                v = tv[k, 0, at, :] + tv[k, 1, at, :] + tv[k, 2, at, :]
                lanes = slice(l * 128, l * 128 + 128)
                yv[k, 8 * b:8 * b + 8, lanes] = (xv[k, 8 * b:8 * b + 8, lanes].astype(F32) + v).astype(BF16)
        store(k).start()
    for k in range(n):
        store(k).wait()


def _final(c, x, terms, y):
    n = TOK // FR
    dma = pltpu.SemaphoreType.DMA
    extra = [] if y is None else [y]
    return pl.pallas_call(
        functools.partial(_final_kernel, c),
        in_specs=[HBM] * (4 + len(extra)),
        out_specs=HBM,
        out_shape=jax.ShapeDtypeStruct((TOK, D), BF16),
        scratch_shapes=[pltpu.VMEM((n, FR, DB), BF16), pltpu.VMEM((n, 3, FR * LT, 128), F32), pltpu.VMEM((n, FR, DB), BF16),
                        dma((n,)), dma((n, 3)), dma((n,))],
        input_output_aliases={4: 0} if extra else {},
        compiler_params=_params(),
        cost_estimate=_cost(TOK * DB * 256, 16 * TOK * DB),
        name="final",
    )(x, *terms, *extra)


def solution(mesh):
    rows = P(("ep", "tp"), None)

    def layer(x, idx, g, slot, ws1, ws3, ws2, w1, w3, w2):
        sub = lax.axis_index("ep") * SUB
        key = jnp.where(slot >= 0, idx * CAP + slot, -1)
        meta = jnp.concatenate([key.astype(F32).T, g.T], axis=0)
        w13 = jnp.concatenate([lax.dynamic_slice(w, (0, sub), (D, SUB)).T for w in (ws1, ws3)], axis=0)
        wq2 = lax.dynamic_slice(ws2, (sub, 0), (SUB, D))
        wq2 = jnp.stack([wq2[:, c * DB:(c + 1) * DB] for c in range(D // DB)])
        h, hs, w2a, w2b, lists = _front(x, meta, w13, wq2, w1, w3)
        w2o = lax.ppermute(w2b, "tp", YSW)
        tok = lists[:, :4].astype(I32).reshape(-1)
        gate = lists[:, 4:8].reshape(-1)

        y = None
        for c in range(D // DB):
            own, near, far, cross = _down(c, tok, gate, hs, wq2, (w2a,) if c == 0 else (w2b, w2o), h, w2)
            cross = lax.ppermute(cross, "ep", CORE)
            near = lax.ppermute(near, "ep", CORE)
            far = lax.ppermute(far + cross, "ep", XSW)
            y = _final(c, x, (own, near, far), y)
        return y

    return jax.shard_map(
        layer, mesh=mesh,
        in_specs=(rows, rows, rows, rows, P(None, "tp"), P(None, "tp"), P("tp", None),
                  P("ep", None, None), P("ep", None, None), P("ep", None, None)),
        out_specs=rows, check_vma=False)
```

time: 975 us -> 379 us (0.39)
  waiting for transfers between devices: 424 us -> 83.1 us
  Pallas kernels: 0 us -> 275 us
  blocking collectives: 198 us -> 0 us
  matrix products: 192 us -> 0 us
  local copies, waits for them, and re-layouts: 105 us -> 6.83 us
  other arithmetic: 25.2 us -> 7.89 us
  between operations: 14 us -> 0.31 us
    pallas_call x0 -> x5, Pallas kernels: none -> 275 us  [the longest x1 169 us: _front(): pl.pallas_call(_front_kernel, in_specs=[HBM] * 6, out_specs=[HBM] * 4 + [...]
    all_gather x1 -> x0, waiting for transfers between devices: 232 us -> none  [body(): xg = lax.all_gather(x, 'tp', axis=0, tiled=True)]
    all_to_all x1 -> x0, blocking collectives: 198 us -> none  [_routed(): recv = lax.all_to_all(send.reshape(ep, el, cap, d), 'ep', 0, 0, tiled=True)]
    dot_general x5 -> x0, matrix products: 192 us -> none  [the longest x1 48.6 us: _experts(): b = jnp.einsum('erd,edf->erf', xs, w3, preferred_element_type=jnp.float32)]
    all_to_all x1 -> x0, waiting for transfers between devices: 192 us -> none  [_routed(): back = lax.all_to_all(out, 'ep', 0, 0, tiled=True).reshape(e * cap, d)]
    ppermute x0 -> x7, waiting for transfers between devices: none -> 83.1 us  [the longest x2 82.7 us: layer(): far = lax.ppermute(far + cross, 'ep', XSW)]
    gather x2 -> x0, local copies, waits for them, and re-layouts: 37.7 us -> none  [_routed(): r = jnp.take(back, jnp.where(kept, pos, 0), axis=0)]
    reshape x3 -> x2, local copies, waits for them, and re-layouts: 29 us -> 1.79 us  [the longest x1 0.9 us: layer(): tok = lists[:, :4].astype(I32).reshape(-1)]
  transfers between devices with their start and end apart: 3 -> 7, of which waited for: 2 -> 3; matrix products, arithmetic and copies ran while one was open for 27% -> 2% of each run, Pallas kernels for 0% -> 27%
where the time goes in v1:
time: 379 us
  Pallas kernels  275 us (73%)
  waiting for transfers between devices  83.1 us (22%)
  other arithmetic  7.89 us (2%)
  local copies, waits for them, and re-layouts  6.83 us (2%)
  starting transfers between devices  5.24 us (1%)
    pallas_call x1, Pallas kernels, _front(): pl.pallas_call(_front_kernel, in_specs=[HBM] * 6, out_specs=[HBM] * 4 + [...  169 us
    pallas_call x2, Pallas kernels, _down(): pl.pallas_call(functools.partial(_down_kernel, c), grid_spec=pltpu.Prefet...  98.3 us
    ppermute x2, waiting for transfers between devices, layer(): far = lax.ppermute(far + cross, 'ep', XSW)  82.7 us
    pallas_call x2, Pallas kernels, _final(): pl.pallas_call(functools.partial(_final_kernel, c), in_specs=[HBM] * (4 +...  8.4 us
  transfers between devices with their start and end apart: 7, of which 3 were waited for; matrix products, arithmetic and copies ran while one was open for 2% of the time, Pallas kernels for 27%

profile of v1, /device:TPU:0, one launch (start us, length us, event | category | flops | bytes accessed | tf_op | source)
XLA Modules:
  0.0 378.7 jit_solution(9149644268314326105)
XLA Ops:
  0.0 1.1 dynamic-slice_bitcast_fusion.3
  1.1 1.0 pad_maximum_fusion.1.wq2.w_own
  2.1 1.5 dynamic-slice_bitcast_fusion
  3.6 0.0 copy-start.6
  3.6 0.0 copy-start.7
  3.6 0.0 copy-start.8
  3.7 1.3 pad_maximum_fusion.w13
  4.9 0.6 pad_maximum_fusion.2.meta
  5.6 168.6 %front.1 = (bf16[15,288,1408]{2,1,0:T(8,128)(2,1)}, bf16[4,2048,384]{2,1,0:T(8,128)(2,1)}, bf16[8,176,1024]{2,1,0:T(8,128)(2,1)}, bf16[4,176,1024]{2,1,0:T(8,128)(2,1)}, f32[1080,128]{1,0:T(8,128)}) custom-call(bf16[512,2048]{1,0:T(8,128)(2,1)} %x.5, f32[8,512]{1,0:T(8,128)} %pad_maximum_fusion.2.meta, bf16[352,2048]{1,0:T(8,128)(2,1)} %pad_maximum_fusion.w13, ...), custom_call_target="tpu_custom_call" | custom-call | flops 75598135296 | bytes 173015040 | tf_op jit(solution)/shard_map/front/pallas_call | solution.py:303
  174.2 1.6 collective-permute-start
  175.7 1.4 fusion
  177.1 0.9 reshape.6.tok
  178.0 0.9 reshape.7.gate
  178.9 49.3 %down.3 = (f32[4104,128]{1,0:T(8,128)}, f32[4104,128]{1,0:T(8,128)}, f32[4104,128]{1,0:T(8,128)}, f32[4104,128]{1,0:T(8,128)}) custom-call(s32[4320]{0:T(1024)} %reshape.6.tok, f32[4320]{0:T(1024)} %reshape.7.gate, bf16[4,2048,384]{2,1,0:T(8,128)(2,1)} %get-tuple-element.19.hs, bf16[2,176,1024]{2,1,0:T(8,128)(2,1)} %pad_maximum_fusion.1.wq2.w_own, ...), custom_call_target="tpu_custom_call" | custom-call | flops 18899533824 | bytes 43253760 | tf_op jit(solution)/shard_map/down/pallas_call | solution.py:421
  228.2 0.1 collective-permute-start.5
  228.3 0.0 copy-start.5
  228.3 1.1 copy-done.5
  229.4 49.1 %down.2 = (f32[4104,128]{1,0:T(8,128)}, f32[4104,128]{1,0:T(8,128)}, f32[4104,128]{1,0:T(8,128)}, f32[4104,128]{1,0:T(8,128)}) custom-call(s32[4320]{0:T(1024)} %reshape.6.tok, f32[4320]{0:T(1024)} %reshape.7.gate, bf16[4,2048,384]{2,1,0:T(8,128)(2,1)} %get-tuple-element.19.hs, bf16[2,176,1024]{2,1,0:T(8,128)(2,1)} %pad_maximum_fusion.1.wq2.w_own, ...), custom_call_target="tpu_custom_call" | custom-call | flops 18899533824 | bytes 43253760 | tf_op jit(solution)/shard_map/down/pallas_call | solution.py:421
  278.5 0.6 collective-permute-start.2
  279.1 0.1 collective-permute-start.4
  279.1 0.0 collective-permute-done.5
  279.1 2.0 add.17
  281.1 1.4 collective-permute-start.6
  282.5 0.2 collective-permute-start.1
  282.7 0.4 collective-permute-done.2
  283.1 1.6 add.16
  284.7 1.4 collective-permute-start.3
  286.1 43.7 %collective-permute-done.6.far = f32[4104,128]{1,0:T(8,128)S(1)} collective-permute-done((f32[4104,128]{1,0:T(8,128)S(1)}, f32[4104,128]{1,0:T(8,128)S(1)}, u32[]{:S(2)}, u32[]{:S(2)}) %collective-permute-start.6) | collective-permute-done | bytes 2101280 | tf_op jit(solution)/shard_map/ppermute | solution.py:511
  329.8 1.3 copy-done.4
  331.1 4.2 %final.2.rest_0_ = bf16[512,2048]{1,0:T(8,128)(2,1)} custom-call(bf16[512,2048]{1,0:T(8,128)(2,1)} %x.5, f32[4104,128]{1,0:T(8,128)} %get-tuple-element.27.own, f32[4104,128]{1,0:T(8,128)} %copy-done.3, f32[4104,128]{1,0:T(8,128)} %copy-done.4), custom_call_target="tpu_custom_call" | custom-call | flops 134217728 | bytes 8388608 | tf_op jit(solution)/shard_map/final/pallas_call | solution.py:477
  335.3 39.1 %collective-permute-done.3.far = f32[4104,128]{1,0:T(8,128)} collective-permute-done((f32[4104,128]{1,0:T(8,128)}, f32[4104,128]{1,0:T(8,128)}, u32[]{:S(2)}, u32[]{:S(2)}) %collective-permute-start.3) | collective-permute-done | bytes 2101280 | tf_op jit(solution)/shard_map/ppermute | solution.py:511
  374.4 4.2 %final.3 = bf16[512,2048]{1,0:T(8,128)(2,1)} custom-call(bf16[512,2048]{1,0:T(8,128)(2,1)} %x.5, f32[4104,128]{1,0:T(8,128)} %get-tuple-element.22.own, f32[4104,128]{1,0:T(8,128)} %copy-done, f32[4104,128]{1,0:T(8,128)} %collective-permute-done.3.far, bf16[512,2048]{1,0:T(8,128)(2,1)} %final.2.rest_0_), custom_call_target="tpu_custom_call", output_to_operand_aliasing={{}: (4, {})} | custom-call | flops 134217728 | bytes 8388608 | tf_op jit(solution)/shard_map/final/pallas_call | solution.py:477
  (16 shorter events, 0.0 us)
Async XLA Ops:
  3.6 1.3 copy-start.6
  3.6 1.3 copy-start.7
  3.6 1.3 copy-start.8
  174.2 54.1 %collective-permute-start = (bf16[4,176,1024]{2,1,0:T(8,128)(2,1)}, bf16[4,176,1024]{2,1,0:T(8,128)(2,1)S(1)}, u32[]{:S(2)}, u32[]{:S(2)}) collective-permute-start(bf16[4,176,1024]{2,1,0:T(8,128)(2,1)} %get-tuple-element.20.rest_0_), channel_id=1, source_target_pairs={{0,4},{4,0},{8,12},{12,8},{16,20},{20,16},{24,28},{28,24},{1,5},{5... | collective-permute-start | bytes 4325384 | tf_op jit(solution)/shard_map/ppermute | solution.py:502
  228.2 50.9 %copy-start.2 = (f32[4104,128]{1,0:T(8,128)S(1)}, f32[4104,128]{1,0:T(8,128)}, u32[]{:S(2)}) copy-start(f32[4104,128]{1,0:T(8,128)} %get-tuple-element.29) | copy-start | bytes 6303748
  228.2 50.9 %collective-permute-start.5 = (f32[4104,128]{1,0:T(8,128)}, f32[4104,128]{1,0:T(8,128)}, u32[]{:S(2)}, u32[]{:S(2)}) collective-permute-start(f32[4104,128]{1,0:T(8,128)} %get-tuple-element.30), channel_id=1, source_target_pairs={{0,1},{1,0},{2,3},{3,2},{4,5},{5,4},{6,7},{7,6},{8,9},{9,8},{10,11... | collective-permute-start | bytes 6303752 | tf_op jit(solution)/shard_map/ppermute | solution.py:509
  228.3 1.1 copy-start.5
  278.5 4.6 %collective-permute-start.2 = (f32[4104,128]{1,0:T(8,128)}, f32[4104,128]{1,0:T(8,128)S(1)}, u32[]{:S(2)}, u32[]{:S(2)}) collective-permute-start(f32[4104,128]{1,0:T(8,128)} %get-tuple-element.25), channel_id=1, source_target_pairs={{0,1},{1,0},{2,3},{3,2},{4,5},{5,4},{6,7},{7,6},{8,9},{9,8},{10,11... | collective-permute-start | bytes 6303752 | tf_op jit(solution)/shard_map/ppermute | solution.py:509
  279.1 7.0 %collective-permute-start.4 = (f32[4104,128]{1,0:T(8,128)}, f32[4104,128]{1,0:T(8,128)S(1)}, u32[]{:S(2)}, u32[]{:S(2)}) collective-permute-start(f32[4104,128]{1,0:T(8,128)} %get-tuple-element.28), channel_id=1, source_target_pairs={{0,1},{1,0},{2,3},{3,2},{4,5},{5,4},{6,7},{7,6},{8,9},{9,8},{10,11... | collective-permute-start | bytes 6303752 | tf_op jit(solution)/shard_map/ppermute | solution.py:510
  279.1 3.9 %copy-start.1 = (f32[4104,128]{1,0:T(8,128)S(1)}, f32[4104,128]{1,0:T(8,128)}, u32[]{:S(2)}) copy-start(f32[4104,128]{1,0:T(8,128)} %get-tuple-element.24) | copy-start | bytes 6303748
  281.1 48.7 %collective-permute-start.6 = (f32[4104,128]{1,0:T(8,128)S(1)}, f32[4104,128]{1,0:T(8,128)S(1)}, u32[]{:S(2)}, u32[]{:S(2)}) collective-permute-start(f32[4104,128]{1,0:T(8,128)S(1)} %add.17), channel_id=1, source_target_pairs={{0,2},{1,3},{2,0},{3,1},{4,6},{5,7},{6,4},{7,5},{8,10},{9,11},{10,... | collective-permute-start | bytes 6303752 | tf_op jit(solution)/shard_map/ppermute | solution.py:511
  282.5 52.7 %collective-permute-start.1 = (f32[4104,128]{1,0:T(8,128)}, f32[4104,128]{1,0:T(8,128)S(1)}, u32[]{:S(2)}, u32[]{:S(2)}) collective-permute-start(f32[4104,128]{1,0:T(8,128)} %get-tuple-element.23), channel_id=1, source_target_pairs={{0,1},{1,0},{2,3},{3,2},{4,5},{5,4},{6,7},{7,6},{8,9},{9,8},{10,11... | collective-permute-start | bytes 6303752 | tf_op jit(solution)/shard_map/ppermute | solution.py:510
  284.7 89.7 %collective-permute-start.3 = (f32[4104,128]{1,0:T(8,128)}, f32[4104,128]{1,0:T(8,128)}, u32[]{:S(2)}, u32[]{:S(2)}) collective-permute-start(f32[4104,128]{1,0:T(8,128)} %add.16), channel_id=1, source_target_pairs={{0,2},{1,3},{2,0},{3,1},{4,6},{5,7},{6,4},{7,5},{8,10},{9,11},{10,... | collective-permute-start | bytes 6303752 | tf_op jit(solution)/shard_map/ppermute | solution.py:511
  286.1 43.7 %copy-start.3 = (f32[4104,128]{1,0:T(8,128)}, f32[4104,128]{1,0:T(8,128)S(1)}, u32[]{:S(2)}) copy-start(f32[4104,128]{1,0:T(8,128)S(1)} %collective-permute-done.4.near) | copy-start | bytes 6303748
  329.8 1.3 copy-start.4
  335.3 39.1 %copy-start = (f32[4104,128]{1,0:T(8,128)}, f32[4104,128]{1,0:T(8,128)S(1)}, u32[]{:S(2)}) copy-start(f32[4104,128]{1,0:T(8,128)S(1)} %collective-permute-done.1.near) | copy-start | bytes 6303748
